TPU v7x, 128 devices: a whole 4x4x4 slice. The times are simulated.
128 devices in a mesh: seq: 16 (over x, y), head: 8 (over z, core).
Axes of the slice: x: 4, y: 4, z: 4, core: 2. Of those that a mesh axis runs over, the one named last changes fastest.
Arguments:
- queries: bfloat16 [4096, 12288], P('seq', 'head'), may hold values from -256 to 256
- own_latent: bfloat16 [4096, 576], P('seq'), may hold values from -16 to 16
- cache: bfloat16 [512, 128, 576], P('seq', 'head'), may hold values from -6 to 6
- block_list: int32 [16, 32], replicated, may hold values from 0 to 511, as said below
- offsets: int32 [16, 32], P('seq'), may hold values from -4096 to 4096
- tile_mask: int32 [16, 2, 32], P('seq'), may hold values 0 or 1
- w_uk: bfloat16 [64, 128, 512], P('head'), may hold values from -0.5 to 0.5
- w_uv: bfloat16 [64, 512, 128], P('head'), may hold values from -0.25 to 0.25
- w_o: bfloat16 [8192, 7168], P('head'), may hold values from -0.0625 to 0.0625
Outputs:
- layer_out: bfloat16 [4096, 7168], P('seq', 'head')
Inputs may be any that keep to these rules, and one draw needn't show every extreme that they name: `block_list`: entry (r, j) names a pooled span whose owner is index entry // 32 of seq. In each row no owner is named more than 4 times, and at least one owner is named exactly 4 times.
All inputs are finite; a program needn't handle non-finite values. No bound on the sum of `tile_mask` on one device may be relied on, other than what follows from the above.
Results may differ from a plain program's by a relative error of at most 0.015.
Values may be sent and summed in bfloat16 or wider, within the bound.
No kernel may reach another device: no remote copies, remote signals or barrier semaphores. Data moves between devices by JAX's collectives and lax.ppermute only.
A program may use at most 128 MiB of HBM per device.

v0:
```python
import jax
import jax.numpy as jnp
from jax import lax
from jax.sharding import PartitionSpec as P

MOST = 4
THETA = 50000.0


def rerotate(blocks, shift, latent_width):
    rotary_width = blocks.shape[-1] - latent_width
    halfway = rotary_width // 2
    inverse = THETA ** (-jnp.arange(halfway, dtype=jnp.float32) * 2.0 / rotary_width)
    angles = shift.astype(jnp.float32)[:, None] * inverse[None, :]
    cosine_table = jnp.cos(angles)[:, None, :]
    sine_table = jnp.sin(angles)[:, None, :]
    rotary = blocks[..., latent_width:].astype(jnp.float32)
    first_half = rotary[..., :halfway]
    second_half = rotary[..., halfway:]
    turned = jnp.concatenate(
        [
            first_half * cosine_table - second_half * sine_table,
            second_half * cosine_table + first_half * sine_table,
        ],
        axis=-1,
    )
    return jnp.concatenate([blocks[..., :latent_width], turned.astype(jnp.bfloat16)], axis=-1)


def allowed_keys(tiles, query_rows, block_rows):
    listed_mask = jnp.repeat(jnp.repeat(tiles > 0, block_rows, axis=0), block_rows, axis=1)
    causal = jnp.tril(jnp.ones((query_rows, query_rows), jnp.bool_))
    return jnp.concatenate([causal, listed_mask], axis=1)


def attend(grouped, context, allowed, key_maps, value_maps):
    nope_width = key_maps.shape[1]
    latent_width = key_maps.shape[2]
    factor = grouped.shape[-1] ** (-0.5)
    value_latent = context[:, :latent_width]

    def one_head(inputs):
        head_query, key_map, value_map = inputs
        query_latent = jnp.dot(
            head_query[:, :nope_width], key_map, preferred_element_type=jnp.float32
        ).astype(jnp.bfloat16)
        query_full = jnp.concatenate([query_latent, head_query[:, nope_width:]], axis=1)
        scores = (
            lax.dot_general(
                query_full, context, (((1,), (1,)), ((), ())), preferred_element_type=jnp.float32
            )
            * factor
        )
        scores = jnp.where(allowed, scores, -1e30)
        highest = jnp.max(scores, axis=1, keepdims=True)
        weights = jnp.exp(scores - highest)
        denominator = jnp.sum(weights, axis=1, keepdims=True)
        shares = (weights / denominator).astype(jnp.bfloat16)
        mixed_latent = jnp.dot(shares, value_latent, preferred_element_type=jnp.float32).astype(
            jnp.bfloat16
        )
        return jnp.dot(mixed_latent, value_map, preferred_element_type=jnp.float32).astype(
            jnp.bfloat16
        )

    per_head = lax.map(one_head, (jnp.transpose(grouped, (1, 0, 2)), key_maps, value_maps))
    return jnp.transpose(per_head, (1, 0, 2)).reshape(grouped.shape[0], -1)


def per_device(queries, own_latent, cache, block_list, offsets, tile_mask, w_uk, w_uv, w_o):
    seq_count = lax.axis_size("seq")
    seq_index = lax.axis_index("seq")
    spans_held = cache.shape[0]
    latent_full = cache.shape[2]
    listed_count = block_list.shape[1]
    owners = block_list // spans_held
    within = block_list % spans_held
    earlier = jnp.tril(jnp.ones((listed_count, listed_count), jnp.bool_), -1)
    same_owner = owners[:, :, None] == owners[:, None, :]
    ranking = jnp.sum(same_owner & earlier[None], axis=2)
    slot_ids = jnp.arange(MOST, dtype=jnp.int32)
    matches = (owners == seq_index)[:, :, None] & (ranking[:, :, None] == slot_ids[None, None, :])
    send_index = jnp.sum(jnp.where(matches, within[:, :, None], 0), axis=1)
    my_owners = lax.dynamic_index_in_dim(owners, seq_index, 0, keepdims=False)
    my_ranking = lax.dynamic_index_in_dim(ranking, seq_index, 0, keepdims=False)
    flat_slot = my_owners * MOST + my_ranking
    arrived = lax.all_to_all(cache[send_index], "seq", split_axis=0, concat_axis=0, tiled=True)
    picked = arrived.reshape(seq_count * MOST, cache.shape[1], latent_full)[flat_slot]
    blocks = lax.all_gather(picked, "head", axis=1, tiled=True)
    latent_width = w_uk.shape[2]
    block_rows = blocks.shape[1]
    turned = rerotate(blocks, offsets[0], latent_width).reshape(
        listed_count * block_rows, latent_full
    )
    context = jnp.concatenate([own_latent, turned], axis=0)
    query_rows = own_latent.shape[0]
    allowed = allowed_keys(tile_mask[0], query_rows, block_rows)
    head_width = w_uk.shape[1] + latent_full - latent_width
    grouped = queries.reshape(query_rows, -1, head_width)
    head_out = attend(grouped, context, allowed, w_uk, w_uv)
    partial_value = jnp.dot(head_out, w_o, preferred_element_type=jnp.float32)
    result = lax.psum_scatter(
        partial_value.astype(jnp.bfloat16), "head", scatter_dimension=1, tiled=True
    )
    return result


def solution(mesh):
    placed = (
        P("seq", "head"),
        P("seq", None),
        P("seq", "head", None),
        P(),
        P("seq", None),
        P("seq", None, None),
        P("head", None, None),
        P("head", None, None),
        P("head", None),
    )
    return jax.shard_map(
        per_device, mesh=mesh, in_specs=placed, out_specs=P("seq", "head"), check_vma=False
    )
```

profile of v0, /device:TPU:0, one launch (start us, length us, event | category | flops | bytes accessed | tf_op | source)
XLA Modules:
  0.0 265.0 jit_solution(6012045879321765092)
XLA Ops:
  10.7 7.3 %all-to-all-start = ((bf16[16,4,16,576]{3,2,1,0:T(8,128)(2,1)}), bf16[16,4,16,576]{3,2,1,0:T(8,128)(2,1)S(1)}, u32[]{:S(2)}, u32[]{:S(2)}) async-start(bf16[16,4,16,576]{3,2,1,0:T(8,128)(2,1)} %bitcast.7), calls=%async_computation | async-start | bytes 2621440 | tf_op jit(solution)/shard_map/all_to_all | solution.py:87
  18.1 20.7 %all-to-all-done = bf16[16,4,16,576]{3,2,1,0:T(8,128)(2,1)S(1)} async-done(((bf16[16,4,16,576]{3,2,1,0:T(8,128)(2,1)}), bf16[16,4,16,576]{3,2,1,0:T(8,128)(2,1)S(1)}, u32[]{:S(2)}, u32[]{:S(2)}) %all-to-all-start) | async-done | bytes 1179680 | tf_op jit(solution)/shard_map/all_to_all | solution.py:87
  45.4 30.7 %all-gather.3.cloned.1.call-done = bf16[32,128,576]{2,1,0:T(8,128)(2,1)} async-done(((bf16[32,16,576]{2,1,0:T(8,128)(2,1)}), bf16[32,128,576]{2,1,0:T(8,128)(2,1)}) %all-gather.3.cloned.1.call-update) | async-done | bytes 4718608 | tf_op jit(solution)/shard_map/all_gather | solution.py:89
  78.4 2.2 slice-done
  81.7 2.9 %pad_maximum_fusion = bf16[4352,576]{1,0:T(8,128)(2,1)} fusion(bf16[256,576]{1,0:T(8,128)(2,1)S(1)} %copy.24, bf16[4096,576]{1,0:T(8,128)(2,1)S(1)} %bitcast.53), kind=kLoop, calls=%fused_computation.28 | loop fusion | flops 10027008 | bytes 10027008 | tf_op jit(solution)/shard_map/concatenate | solution.py:95
  84.7 2.5 fusion.18
  87.1 115.0 %while.10 = (s32[]{:T(128)}, bf16[8,256,128]{1,2,0:T(8,128)(2,1)S(1)}, bf16[8,256,192]{1,2,0:T(8,128)(2,1)S(1)}, bf16[8,128,512]{2,1,0:T(8,128)(2,1)}, bf16[4352...) while((s32[]{:T(128)}, ...), condition=%wide.region_5.6_spmd, body=%wide.region_2.5_spmd.sunk | while | flops 2501213696 | bytes 43456640 | solution.py:66
  88.4 4.9 %fusion.41 = (f32[256]{0:T(256)S(1)}, f32[256,4352]{1,0:T(8,128)S(1)}) fusion(pred[256,4352]{1,0:T(32,128)(4,1)} %get-tuple-element.172, bf16[4352,576]{1,0:T(8,128)(2,1)} %get-tuple-element.171, bf16[256,64]{1,0:T(8,128)(2,1)S(1)} %slice.54, bf16[256,512]{1,0:T(8,128)(2,1)S(1)} %convolution_convert_fusion.3), kind=kOutput, calls=%fused_computation.63.clone.1 | convolution fusion | flops 1287388928 | bytes 10880000 | tf_op jit(solution)/shard_map/while/body/eval_jaxpr/dot_general | solution.py:49
  93.3 2.1 copy-done.2
  96.2 5.1 %fusion.43 = bf16[1,256,128]{2,1,0:T(8,128)(2,1)S(1)} fusion(bf16[4352,512]{1,0:T(8,128)(2,1)} %get-tuple-element.173, f32[256,4352]{1,0:T(8,128)} %copy-done.2, f32[256]{0:T(256)S(1)} %fusion.42, f32[256]{0:T(256)S(1)} %get-tuple-element.148, bf16[8,512,128]{2,1,0:T(8,128)(2,1)} %get-tuple-element.174, s32[]{:T(128)} %get-tuple-element.158), kind=kOutput, calls=%fused_computation.12.clone.1 | convolution fusion | flops 1177911296 | bytes 9112064 | tf_op jit(solution)/shard_map/while/body/eval_jaxpr/dot_general | solution.py:62
  102.8 4.9 %fusion.41 = (f32[256]{0:T(256)S(1)}, f32[256,4352]{1,0:T(8,128)S(1)}) fusion(pred[256,4352]{1,0:T(32,128)(4,1)} %get-tuple-element.172, bf16[4352,576]{1,0:T(8,128)(2,1)} %get-tuple-element.171, bf16[256,64]{1,0:T(8,128)(2,1)S(1)} %slice.54, bf16[256,512]{1,0:T(8,128)(2,1)S(1)} %convolution_convert_fusion.3), kind=kOutput, calls=%fused_computation.63.clone.1 | convolution fusion | flops 1287388928 | bytes 10880000 | tf_op jit(solution)/shard_map/while/body/eval_jaxpr/dot_general | solution.py:49
  107.7 2.1 copy-done.2
  110.6 5.1 %fusion.43 = bf16[1,256,128]{2,1,0:T(8,128)(2,1)S(1)} fusion(bf16[4352,512]{1,0:T(8,128)(2,1)} %get-tuple-element.173, f32[256,4352]{1,0:T(8,128)} %copy-done.2, f32[256]{0:T(256)S(1)} %fusion.42, f32[256]{0:T(256)S(1)} %get-tuple-element.148, bf16[8,512,128]{2,1,0:T(8,128)(2,1)} %get-tuple-element.174, s32[]{:T(128)} %get-tuple-element.158), kind=kOutput, calls=%fused_computation.12.clone.1 | convolution fusion | flops 1177911296 | bytes 9112064 | tf_op jit(solution)/shard_map/while/body/eval_jaxpr/dot_general | solution.py:62
  117.2 4.9 %fusion.41 = (f32[256]{0:T(256)S(1)}, f32[256,4352]{1,0:T(8,128)S(1)}) fusion(pred[256,4352]{1,0:T(32,128)(4,1)} %get-tuple-element.172, bf16[4352,576]{1,0:T(8,128)(2,1)} %get-tuple-element.171, bf16[256,64]{1,0:T(8,128)(2,1)S(1)} %slice.54, bf16[256,512]{1,0:T(8,128)(2,1)S(1)} %convolution_convert_fusion.3), kind=kOutput, calls=%fused_computation.63.clone.1 | convolution fusion | flops 1287388928 | bytes 10880000 | tf_op jit(solution)/shard_map/while/body/eval_jaxpr/dot_general | solution.py:49
  122.1 2.1 copy-done.2
  125.0 5.1 %fusion.43 = bf16[1,256,128]{2,1,0:T(8,128)(2,1)S(1)} fusion(bf16[4352,512]{1,0:T(8,128)(2,1)} %get-tuple-element.173, f32[256,4352]{1,0:T(8,128)} %copy-done.2, f32[256]{0:T(256)S(1)} %fusion.42, f32[256]{0:T(256)S(1)} %get-tuple-element.148, bf16[8,512,128]{2,1,0:T(8,128)(2,1)} %get-tuple-element.174, s32[]{:T(128)} %get-tuple-element.158), kind=kOutput, calls=%fused_computation.12.clone.1 | convolution fusion | flops 1177911296 | bytes 9112064 | tf_op jit(solution)/shard_map/while/body/eval_jaxpr/dot_general | solution.py:62
  131.5 4.9 %fusion.41 = (f32[256]{0:T(256)S(1)}, f32[256,4352]{1,0:T(8,128)S(1)}) fusion(pred[256,4352]{1,0:T(32,128)(4,1)} %get-tuple-element.172, bf16[4352,576]{1,0:T(8,128)(2,1)} %get-tuple-element.171, bf16[256,64]{1,0:T(8,128)(2,1)S(1)} %slice.54, bf16[256,512]{1,0:T(8,128)(2,1)S(1)} %convolution_convert_fusion.3), kind=kOutput, calls=%fused_computation.63.clone.1 | convolution fusion | flops 1287388928 | bytes 10880000 | tf_op jit(solution)/shard_map/while/body/eval_jaxpr/dot_general | solution.py:49
  136.5 2.1 copy-done.2
  139.4 5.1 %fusion.43 = bf16[1,256,128]{2,1,0:T(8,128)(2,1)S(1)} fusion(bf16[4352,512]{1,0:T(8,128)(2,1)} %get-tuple-element.173, f32[256,4352]{1,0:T(8,128)} %copy-done.2, f32[256]{0:T(256)S(1)} %fusion.42, f32[256]{0:T(256)S(1)} %get-tuple-element.148, bf16[8,512,128]{2,1,0:T(8,128)(2,1)} %get-tuple-element.174, s32[]{:T(128)} %get-tuple-element.158), kind=kOutput, calls=%fused_computation.12.clone.1 | convolution fusion | flops 1177911296 | bytes 9112064 | tf_op jit(solution)/shard_map/while/body/eval_jaxpr/dot_general | solution.py:62
  145.9 4.9 %fusion.41 = (f32[256]{0:T(256)S(1)}, f32[256,4352]{1,0:T(8,128)S(1)}) fusion(pred[256,4352]{1,0:T(32,128)(4,1)} %get-tuple-element.172, bf16[4352,576]{1,0:T(8,128)(2,1)} %get-tuple-element.171, bf16[256,64]{1,0:T(8,128)(2,1)S(1)} %slice.54, bf16[256,512]{1,0:T(8,128)(2,1)S(1)} %convolution_convert_fusion.3), kind=kOutput, calls=%fused_computation.63.clone.1 | convolution fusion | flops 1287388928 | bytes 10880000 | tf_op jit(solution)/shard_map/while/body/eval_jaxpr/dot_general | solution.py:49
  153.7 5.1 %fusion.43 = bf16[1,256,128]{2,1,0:T(8,128)(2,1)S(1)} fusion(bf16[4352,512]{1,0:T(8,128)(2,1)} %get-tuple-element.173, f32[256,4352]{1,0:T(8,128)} %copy-done.2, f32[256]{0:T(256)S(1)} %fusion.42, f32[256]{0:T(256)S(1)} %get-tuple-element.148, bf16[8,512,128]{2,1,0:T(8,128)(2,1)} %get-tuple-element.174, s32[]{:T(128)} %get-tuple-element.158), kind=kOutput, calls=%fused_computation.12.clone.1 | convolution fusion | flops 1177911296 | bytes 9112064 | tf_op jit(solution)/shard_map/while/body/eval_jaxpr/dot_general | solution.py:62
  160.3 4.9 %fusion.41 = (f32[256]{0:T(256)S(1)}, f32[256,4352]{1,0:T(8,128)S(1)}) fusion(pred[256,4352]{1,0:T(32,128)(4,1)} %get-tuple-element.172, bf16[4352,576]{1,0:T(8,128)(2,1)} %get-tuple-element.171, bf16[256,64]{1,0:T(8,128)(2,1)S(1)} %slice.54, bf16[256,512]{1,0:T(8,128)(2,1)S(1)} %convolution_convert_fusion.3), kind=kOutput, calls=%fused_computation.63.clone.1 | convolution fusion | flops 1287388928 | bytes 10880000 | tf_op jit(solution)/shard_map/while/body/eval_jaxpr/dot_general | solution.py:49
  165.3 2.1 copy-done.2
  168.1 5.1 %fusion.43 = bf16[1,256,128]{2,1,0:T(8,128)(2,1)S(1)} fusion(bf16[4352,512]{1,0:T(8,128)(2,1)} %get-tuple-element.173, f32[256,4352]{1,0:T(8,128)} %copy-done.2, f32[256]{0:T(256)S(1)} %fusion.42, f32[256]{0:T(256)S(1)} %get-tuple-element.148, bf16[8,512,128]{2,1,0:T(8,128)(2,1)} %get-tuple-element.174, s32[]{:T(128)} %get-tuple-element.158), kind=kOutput, calls=%fused_computation.12.clone.1 | convolution fusion | flops 1177911296 | bytes 9112064 | tf_op jit(solution)/shard_map/while/body/eval_jaxpr/dot_general | solution.py:62
  174.7 4.9 %fusion.41 = (f32[256]{0:T(256)S(1)}, f32[256,4352]{1,0:T(8,128)S(1)}) fusion(pred[256,4352]{1,0:T(32,128)(4,1)} %get-tuple-element.172, bf16[4352,576]{1,0:T(8,128)(2,1)} %get-tuple-element.171, bf16[256,64]{1,0:T(8,128)(2,1)S(1)} %slice.54, bf16[256,512]{1,0:T(8,128)(2,1)S(1)} %convolution_convert_fusion.3), kind=kOutput, calls=%fused_computation.63.clone.1 | convolution fusion | flops 1287388928 | bytes 10880000 | tf_op jit(solution)/shard_map/while/body/eval_jaxpr/dot_general | solution.py:49
  179.6 2.1 copy-done.2
  182.5 5.1 %fusion.43 = bf16[1,256,128]{2,1,0:T(8,128)(2,1)S(1)} fusion(bf16[4352,512]{1,0:T(8,128)(2,1)} %get-tuple-element.173, f32[256,4352]{1,0:T(8,128)} %copy-done.2, f32[256]{0:T(256)S(1)} %fusion.42, f32[256]{0:T(256)S(1)} %get-tuple-element.148, bf16[8,512,128]{2,1,0:T(8,128)(2,1)} %get-tuple-element.174, s32[]{:T(128)} %get-tuple-element.158), kind=kOutput, calls=%fused_computation.12.clone.1 | convolution fusion | flops 1177911296 | bytes 9112064 | tf_op jit(solution)/shard_map/while/body/eval_jaxpr/dot_general | solution.py:62
  189.1 4.9 %fusion.41 = (f32[256]{0:T(256)S(1)}, f32[256,4352]{1,0:T(8,128)S(1)}) fusion(pred[256,4352]{1,0:T(32,128)(4,1)} %get-tuple-element.172, bf16[4352,576]{1,0:T(8,128)(2,1)} %get-tuple-element.171, bf16[256,64]{1,0:T(8,128)(2,1)S(1)} %slice.54, bf16[256,512]{1,0:T(8,128)(2,1)S(1)} %convolution_convert_fusion.3), kind=kOutput, calls=%fused_computation.63.clone.1 | convolution fusion | flops 1287388928 | bytes 10880000 | tf_op jit(solution)/shard_map/while/body/eval_jaxpr/dot_general | solution.py:49
  196.9 5.1 %fusion.43 = bf16[1,256,128]{2,1,0:T(8,128)(2,1)S(1)} fusion(bf16[4352,512]{1,0:T(8,128)(2,1)} %get-tuple-element.173, f32[256,4352]{1,0:T(8,128)} %copy-done.2, f32[256]{0:T(256)S(1)} %fusion.42, f32[256]{0:T(256)S(1)} %get-tuple-element.148, bf16[8,512,128]{2,1,0:T(8,128)(2,1)} %get-tuple-element.174, s32[]{:T(128)} %get-tuple-element.158), kind=kOutput, calls=%fused_computation.12.clone.1 | convolution fusion | flops 1177911296 | bytes 9112064 | tf_op jit(solution)/shard_map/while/body/eval_jaxpr/dot_general | solution.py:62
  202.2 10.9 %convolution_convert_fusion.1 = bf16[256,7168]{1,0:T(8,128)(2,1)} fusion(bf16[256,1024]{0,1:T(8,128)(2,1)S(1)} %bitcast.62, bf16[1024,7168]{1,0:T(8,128)(2,1)} %param.19), kind=kOutput, calls=%fused_computation.26 | convolution fusion | flops 3759931392 | bytes 18874368 | tf_op jit(solution)/shard_map/dot_general | solution.py:101
  213.1 5.9 %copy.27 = bf16[256,7168]{0,1:T(8,128)(2,1)} copy(bf16[256,7168]{1,0:T(8,128)(2,1)} %convolution_convert_fusion.1) | data formatting | bytes 7340032
  219.0 37.2 %reduce-scatter.4.cloned.1.call-done = bf16[896,256]{1,0:T(8,128)(2,1)} async-done(((bf16[7168,256]{1,0:T(8,128)(2,1)}), bf16[896,256]{1,0:T(8,128)(2,1)}) %reduce-scatter.4.cloned.1.call-update) | async-done | bytes 458768
  (115 shorter events, 37.2 us)
Async XLA Ops:
  6.5 2.4 copy-start
  6.5 33.9 %copy-start.5 = (bf16[256,576]{0,1:T(8,128)(2,1)S(1)}, bf16[256,576]{0,1:T(8,128)(2,1)}, u32[]{:S(2)}) copy-start(bf16[256,576]{0,1:T(8,128)(2,1)} %param.12) | copy-start | bytes 884740
  6.5 34.1 %copy-start.6 = (s32[1,2,32]{2,1,0:T(2,128)S(1)}, s32[1,2,32]{2,1,0:T(2,128)}, u32[]{:S(2)}) copy-start(s32[1,2,32]{2,1,0:T(2,128)} %param.16) | copy-start | bytes 772
  10.7 32.7 %copy-start.3 = (bf16[256,1536]{1,0:T(8,128)(2,1)S(1)}, bf16[256,1536]{1,0:T(8,128)(2,1)}, u32[]{:S(2)}) copy-start(bf16[256,1536]{1,0:T(8,128)(2,1)} %param.11) | copy-start | bytes 2359300
  10.7 33.1 %copy-start.7 = (s32[1,32]{1,0:T(1,128)S(1)}, s32[1,32]{1,0:T(1,128)}, u32[]{:S(2)}) copy-start(s32[1,32]{1,0:T(1,128)} %param.15) | copy-start | bytes 388
  10.7 28.1 %all-to-all-start = ((bf16[16,4,16,576]{3,2,1,0:T(8,128)(2,1)}), bf16[16,4,16,576]{3,2,1,0:T(8,128)(2,1)S(1)}, u32[]{:S(2)}, u32[]{:S(2)}) async-start(bf16[16,4,16,576]{3,2,1,0:T(8,128)(2,1)} %bitcast.7), calls=%async_computation | async-start | bytes 2621440 | tf_op jit(solution)/shard_map/all_to_all | solution.py:87
  18.0 58.0 %all-gather.3.cloned.1.call-start = ((), (), s32[]{:S(2)}) async-start(), calls=%async_computation.2 | async-start | bytes 5898240 | tf_op jit(solution)/shard_map/all_gather | solution.py:89
  40.3 215.9 %reduce-scatter.4.cloned.1.call-start = ((), (), s32[]{:S(2)}) async-start(), calls=%async_computation.3 | async-start | bytes 4128768
  78.4 2.2 slice-start
  84.7 2.5 copy-start.4
  93.3 2.1 copy-start.2
  107.7 2.1 copy-start.2
  122.1 2.1 copy-start.2
  136.5 2.1 copy-start.2
  150.9 2.1 copy-start.2
  165.2 2.1 copy-start.2
  179.6 2.1 copy-start.2
  194.0 2.1 copy-start.2
  202.2 56.0 %copy-start.1 = (bf16[32,16,576]{2,1,0:T(8,128)(2,1)S(1)}, bf16[32,16,576]{2,1,0:T(8,128)(2,1)}, u32[]{:S(2)}) copy-start(bf16[32,16,576]{2,1,0:T(8,128)(2,1)} %param.13) | copy-start | bytes 1769476
Sparse Core Ops, SparseCore 0:
  40.5 35.5 all-gather.2
  219.1 37.0 reduce-scatter.3
where the time goes:
time: 266 us; the launch traced here: 265 us
  matrix products  100 us (38%)
  waiting for transfers between devices  88.6 us (33%)
  local copies, waits for them, and re-layouts  35.9 us (13%)
  other arithmetic  18.6 us (7%)
  between operations  13.6 us (5%)
  starting transfers between devices  7.36 us (3%)
    dot_general x8, matrix products, one_head(): jnp.dot(mixed_latent, value_map, preferred_element_type=jnp.float32)  41.1 us
    dot_general x8, matrix products, one_head(): lax.dot_general(query_full, context, (((1,), (1,)), ((), ())), preferred_...  39.5 us
    unnamed x3, waiting for transfers between devices  37.2 us
    all_gather x1, waiting for transfers between devices, per_device(): blocks = lax.all_gather(picked, 'head', axis=1, tiled=True)  30.7 us
    all_to_all x1, waiting for transfers between devices, per_device(): lax.all_to_all(cache[send_index], 'seq', split_axis=0, concat_axis=0, til...  20.7 us
    while x16, local copies, waits for them, and re-layouts  17.1 us
    dot_general x1, matrix products, per_device(): partial_value = jnp.dot(head_out, w_o, preferred_element_type=jnp.float32)  10.9 us
    unnamed x19, local copies, waits for them, and re-layouts  9.16 us
  transfers between devices with their start and end apart: 3, of which 3 were waited for; matrix products, arithmetic and copies ran while one was open for 2% of the time, Pallas kernels for 0%

commit v1 on v0

--- a/solution.py
+++ b/solution.py
@@ -86,7 +86,8 @@
     flat_slot = my_owners * MOST + my_ranking
     arrived = lax.all_to_all(cache[send_index], "seq", split_axis=0, concat_axis=0, tiled=True)
     picked = arrived.reshape(seq_count * MOST, cache.shape[1], latent_full)[flat_slot]
-    blocks = lax.all_gather(picked, "head", axis=1, tiled=True)
+    pieces = lax.all_gather(picked, "head")
+    blocks = jnp.concatenate(pieces, axis=1)
     latent_width = w_uk.shape[2]
     block_rows = blocks.shape[1]
     turned = rerotate(blocks, offsets[0], latent_width).reshape(

time: 266 us -> 266 us (level)
    reshape x0 -> x1, local copies, waits for them, and re-layouts: none -> 3.29 us  [per_device(): blocks = jnp.concatenate(pieces, axis=1)]
where the time goes in v1:
time: 266 us; the launch traced here: 265 us
  matrix products  100 us (38%)
  waiting for transfers between devices  88.6 us (33%)
  local copies, waits for them, and re-layouts  37.3 us (14%)
  other arithmetic  17.4 us (7%)
  between operations  13.6 us (5%)
  starting transfers between devices  7.36 us (3%)
    dot_general x8, matrix products, one_head(): jnp.dot(mixed_latent, value_map, preferred_element_type=jnp.float32)  41.1 us
    dot_general x8, matrix products, one_head(): lax.dot_general(query_full, context, (((1,), (1,)), ((), ())), preferred_...  39.5 us
    unnamed x3, waiting for transfers between devices  37.2 us
    all_gather x1, waiting for transfers between devices, per_device(): pieces = lax.all_gather(picked, 'head')  30.7 us
    all_to_all x1, waiting for transfers between devices, per_device(): lax.all_to_all(cache[send_index], 'seq', split_axis=0, concat_axis=0, til...  20.7 us
    while x16, local copies, waits for them, and re-layouts  17 us
    dot_general x1, matrix products, per_device(): partial_value = jnp.dot(head_out, w_o, preferred_element_type=jnp.float32)  11 us
    unnamed x19, local copies, waits for them, and re-layouts  9.15 us
  transfers between devices with their start and end apart: 3, of which 3 were waited for; matrix products, arithmetic and copies ran while one was open for 2% of the time, Pallas kernels for 0%

profile of v1, /device:TPU:0, one launch (start us, length us, event | category | flops | bytes accessed | tf_op | source)
XLA Modules:
  0.0 265.5 jit_solution(8601492594841205187)
XLA Ops:
  10.7 7.3 %all-to-all-start = ((bf16[16,4,16,576]{3,2,1,0:T(8,128)(2,1)}), bf16[16,4,16,576]{3,2,1,0:T(8,128)(2,1)S(1)}, u32[]{:S(2)}, u32[]{:S(2)}) async-start(bf16[16,4,16,576]{3,2,1,0:T(8,128)(2,1)} %bitcast.7), calls=%async_computation | async-start | bytes 2621440 | tf_op jit(solution)/shard_map/all_to_all | solution.py:87
  18.1 20.7 %all-to-all-done = bf16[16,4,16,576]{3,2,1,0:T(8,128)(2,1)S(1)} async-done(((bf16[16,4,16,576]{3,2,1,0:T(8,128)(2,1)}), bf16[16,4,16,576]{3,2,1,0:T(8,128)(2,1)S(1)}, u32[]{:S(2)}, u32[]{:S(2)}) %all-to-all-start) | async-done | bytes 1179680 | tf_op jit(solution)/shard_map/all_to_all | solution.py:87
  45.4 30.7 %all-gather.3.cloned.1.call-done = bf16[256,16,576]{2,1,0:T(8,128)(2,1)} async-done(((bf16[32,16,576]{2,1,0:T(8,128)(2,1)}), bf16[256,16,576]{2,1,0:T(8,128)(2,1)}) %all-gather.3.cloned.1.call-update) | async-done | bytes 4718608 | tf_op jit(solution)/shard_map/all_gather | solution.py:89
  76.1 3.3 %copy.31 = bf16[32,8,16,576]{3,2,1,0:T(8,128)(2,1)S(1)} copy(bf16[32,8,16,576]{3,2,0,1:T(8,128)(2,1)} %bitcast.64) | data formatting | bytes 9437184 | tf_op jit(solution)/shard_map/reshape | solution.py:90
  82.1 3.0 %pad_maximum_fusion = bf16[4352,576]{1,0:T(8,128)(2,1)} fusion(bf16[256,576]{1,0:T(8,128)(2,1)S(1)} %copy.32, bf16[4096,576]{1,0:T(8,128)(2,1)S(1)} %bitcast.57), kind=kLoop, calls=%fused_computation.28 | loop fusion | flops 10027008 | bytes 10027008 | tf_op jit(solution)/shard_map/concatenate | solution.py:96
  85.0 2.5 fusion.18
  87.5 115.0 %while.10 = (s32[]{:T(128)}, bf16[8,256,128]{1,2,0:T(8,128)(2,1)S(1)}, bf16[8,256,192]{1,2,0:T(8,128)(2,1)S(1)}, bf16[8,128,512]{2,1,0:T(8,128)(2,1)}, bf16[4352...) while((s32[]{:T(128)}, ...), condition=%wide.region_5.6_spmd, body=%wide.region_2.5_spmd.sunk | while | flops 2501213696 | bytes 43456640 | solution.py:66
  88.8 4.9 %fusion.41 = (f32[256]{0:T(256)S(1)}, f32[256,4352]{1,0:T(8,128)S(1)}) fusion(pred[256,4352]{1,0:T(32,128)(4,1)} %get-tuple-element.180, bf16[4352,576]{1,0:T(8,128)(2,1)} %get-tuple-element.179, bf16[256,64]{1,0:T(8,128)(2,1)S(1)} %slice.54, bf16[256,512]{1,0:T(8,128)(2,1)S(1)} %convolution_convert_fusion.3), kind=kOutput, calls=%fused_computation.63.clone.1 | convolution fusion | flops 1287388928 | bytes 10880000 | tf_op jit(solution)/shard_map/while/body/eval_jaxpr/dot_general | solution.py:49
  93.7 2.1 copy-done.2
  96.6 5.1 %fusion.43 = bf16[1,256,128]{2,1,0:T(8,128)(2,1)S(1)} fusion(bf16[4352,512]{1,0:T(8,128)(2,1)} %get-tuple-element.181, f32[256,4352]{1,0:T(8,128)} %copy-done.2, f32[256]{0:T(256)S(1)} %fusion.42, f32[256]{0:T(256)S(1)} %get-tuple-element.156, bf16[8,512,128]{2,1,0:T(8,128)(2,1)} %get-tuple-element.182, s32[]{:T(128)} %get-tuple-element.166), kind=kOutput, calls=%fused_computation.12.clone.1 | convolution fusion | flops 1177911296 | bytes 9112064 | tf_op jit(solution)/shard_map/while/body/eval_jaxpr/dot_general | solution.py:62
  103.2 4.9 %fusion.41 = (f32[256]{0:T(256)S(1)}, f32[256,4352]{1,0:T(8,128)S(1)}) fusion(pred[256,4352]{1,0:T(32,128)(4,1)} %get-tuple-element.180, bf16[4352,576]{1,0:T(8,128)(2,1)} %get-tuple-element.179, bf16[256,64]{1,0:T(8,128)(2,1)S(1)} %slice.54, bf16[256,512]{1,0:T(8,128)(2,1)S(1)} %convolution_convert_fusion.3), kind=kOutput, calls=%fused_computation.63.clone.1 | convolution fusion | flops 1287388928 | bytes 10880000 | tf_op jit(solution)/shard_map/while/body/eval_jaxpr/dot_general | solution.py:49
  111.0 5.1 %fusion.43 = bf16[1,256,128]{2,1,0:T(8,128)(2,1)S(1)} fusion(bf16[4352,512]{1,0:T(8,128)(2,1)} %get-tuple-element.181, f32[256,4352]{1,0:T(8,128)} %copy-done.2, f32[256]{0:T(256)S(1)} %fusion.42, f32[256]{0:T(256)S(1)} %get-tuple-element.156, bf16[8,512,128]{2,1,0:T(8,128)(2,1)} %get-tuple-element.182, s32[]{:T(128)} %get-tuple-element.166), kind=kOutput, calls=%fused_computation.12.clone.1 | convolution fusion | flops 1177911296 | bytes 9112064 | tf_op jit(solution)/shard_map/while/body/eval_jaxpr/dot_general | solution.py:62
  117.5 4.9 %fusion.41 = (f32[256]{0:T(256)S(1)}, f32[256,4352]{1,0:T(8,128)S(1)}) fusion(pred[256,4352]{1,0:T(32,128)(4,1)} %get-tuple-element.180, bf16[4352,576]{1,0:T(8,128)(2,1)} %get-tuple-element.179, bf16[256,64]{1,0:T(8,128)(2,1)S(1)} %slice.54, bf16[256,512]{1,0:T(8,128)(2,1)S(1)} %convolution_convert_fusion.3), kind=kOutput, calls=%fused_computation.63.clone.1 | convolution fusion | flops 1287388928 | bytes 10880000 | tf_op jit(solution)/shard_map/while/body/eval_jaxpr/dot_general | solution.py:49
  122.5 2.1 copy-done.2
  125.3 5.1 %fusion.43 = bf16[1,256,128]{2,1,0:T(8,128)(2,1)S(1)} fusion(bf16[4352,512]{1,0:T(8,128)(2,1)} %get-tuple-element.181, f32[256,4352]{1,0:T(8,128)} %copy-done.2, f32[256]{0:T(256)S(1)} %fusion.42, f32[256]{0:T(256)S(1)} %get-tuple-element.156, bf16[8,512,128]{2,1,0:T(8,128)(2,1)} %get-tuple-element.182, s32[]{:T(128)} %get-tuple-element.166), kind=kOutput, calls=%fused_computation.12.clone.1 | convolution fusion | flops 1177911296 | bytes 9112064 | tf_op jit(solution)/shard_map/while/body/eval_jaxpr/dot_general | solution.py:62
  131.9 4.9 %fusion.41 = (f32[256]{0:T(256)S(1)}, f32[256,4352]{1,0:T(8,128)S(1)}) fusion(pred[256,4352]{1,0:T(32,128)(4,1)} %get-tuple-element.180, bf16[4352,576]{1,0:T(8,128)(2,1)} %get-tuple-element.179, bf16[256,64]{1,0:T(8,128)(2,1)S(1)} %slice.54, bf16[256,512]{1,0:T(8,128)(2,1)S(1)} %convolution_convert_fusion.3), kind=kOutput, calls=%fused_computation.63.clone.1 | convolution fusion | flops 1287388928 | bytes 10880000 | tf_op jit(solution)/shard_map/while/body/eval_jaxpr/dot_general | solution.py:49
  136.8 2.1 copy-done.2
  139.7 5.1 %fusion.43 = bf16[1,256,128]{2,1,0:T(8,128)(2,1)S(1)} fusion(bf16[4352,512]{1,0:T(8,128)(2,1)} %get-tuple-element.181, f32[256,4352]{1,0:T(8,128)} %copy-done.2, f32[256]{0:T(256)S(1)} %fusion.42, f32[256]{0:T(256)S(1)} %get-tuple-element.156, bf16[8,512,128]{2,1,0:T(8,128)(2,1)} %get-tuple-element.182, s32[]{:T(128)} %get-tuple-element.166), kind=kOutput, calls=%fused_computation.12.clone.1 | convolution fusion | flops 1177911296 | bytes 9112064 | tf_op jit(solution)/shard_map/while/body/eval_jaxpr/dot_general | solution.py:62
  146.3 4.9 %fusion.41 = (f32[256]{0:T(256)S(1)}, f32[256,4352]{1,0:T(8,128)S(1)}) fusion(pred[256,4352]{1,0:T(32,128)(4,1)} %get-tuple-element.180, bf16[4352,576]{1,0:T(8,128)(2,1)} %get-tuple-element.179, bf16[256,64]{1,0:T(8,128)(2,1)S(1)} %slice.54, bf16[256,512]{1,0:T(8,128)(2,1)S(1)} %convolution_convert_fusion.3), kind=kOutput, calls=%fused_computation.63.clone.1 | convolution fusion | flops 1287388928 | bytes 10880000 | tf_op jit(solution)/shard_map/while/body/eval_jaxpr/dot_general | solution.py:49
  154.1 5.1 %fusion.43 = bf16[1,256,128]{2,1,0:T(8,128)(2,1)S(1)} fusion(bf16[4352,512]{1,0:T(8,128)(2,1)} %get-tuple-element.181, f32[256,4352]{1,0:T(8,128)} %copy-done.2, f32[256]{0:T(256)S(1)} %fusion.42, f32[256]{0:T(256)S(1)} %get-tuple-element.156, bf16[8,512,128]{2,1,0:T(8,128)(2,1)} %get-tuple-element.182, s32[]{:T(128)} %get-tuple-element.166), kind=kOutput, calls=%fused_computation.12.clone.1 | convolution fusion | flops 1177911296 | bytes 9112064 | tf_op jit(solution)/shard_map/while/body/eval_jaxpr/dot_general | solution.py:62
  160.6 4.9 %fusion.41 = (f32[256]{0:T(256)S(1)}, f32[256,4352]{1,0:T(8,128)S(1)}) fusion(pred[256,4352]{1,0:T(32,128)(4,1)} %get-tuple-element.180, bf16[4352,576]{1,0:T(8,128)(2,1)} %get-tuple-element.179, bf16[256,64]{1,0:T(8,128)(2,1)S(1)} %slice.54, bf16[256,512]{1,0:T(8,128)(2,1)S(1)} %convolution_convert_fusion.3), kind=kOutput, calls=%fused_computation.63.clone.1 | convolution fusion | flops 1287388928 | bytes 10880000 | tf_op jit(solution)/shard_map/while/body/eval_jaxpr/dot_general | solution.py:49
  165.6 2.1 copy-done.2
  168.5 5.1 %fusion.43 = bf16[1,256,128]{2,1,0:T(8,128)(2,1)S(1)} fusion(bf16[4352,512]{1,0:T(8,128)(2,1)} %get-tuple-element.181, f32[256,4352]{1,0:T(8,128)} %copy-done.2, f32[256]{0:T(256)S(1)} %fusion.42, f32[256]{0:T(256)S(1)} %get-tuple-element.156, bf16[8,512,128]{2,1,0:T(8,128)(2,1)} %get-tuple-element.182, s32[]{:T(128)} %get-tuple-element.166), kind=kOutput, calls=%fused_computation.12.clone.1 | convolution fusion | flops 1177911296 | bytes 9112064 | tf_op jit(solution)/shard_map/while/body/eval_jaxpr/dot_general | solution.py:62
  175.0 4.9 %fusion.41 = (f32[256]{0:T(256)S(1)}, f32[256,4352]{1,0:T(8,128)S(1)}) fusion(pred[256,4352]{1,0:T(32,128)(4,1)} %get-tuple-element.180, bf16[4352,576]{1,0:T(8,128)(2,1)} %get-tuple-element.179, bf16[256,64]{1,0:T(8,128)(2,1)S(1)} %slice.54, bf16[256,512]{1,0:T(8,128)(2,1)S(1)} %convolution_convert_fusion.3), kind=kOutput, calls=%fused_computation.63.clone.1 | convolution fusion | flops 1287388928 | bytes 10880000 | tf_op jit(solution)/shard_map/while/body/eval_jaxpr/dot_general | solution.py:49
  180.0 2.1 copy-done.2
  182.8 5.1 %fusion.43 = bf16[1,256,128]{2,1,0:T(8,128)(2,1)S(1)} fusion(bf16[4352,512]{1,0:T(8,128)(2,1)} %get-tuple-element.181, f32[256,4352]{1,0:T(8,128)} %copy-done.2, f32[256]{0:T(256)S(1)} %fusion.42, f32[256]{0:T(256)S(1)} %get-tuple-element.156, bf16[8,512,128]{2,1,0:T(8,128)(2,1)} %get-tuple-element.182, s32[]{:T(128)} %get-tuple-element.166), kind=kOutput, calls=%fused_computation.12.clone.1 | convolution fusion | flops 1177911296 | bytes 9112064 | tf_op jit(solution)/shard_map/while/body/eval_jaxpr/dot_general | solution.py:62
  189.4 4.9 %fusion.41 = (f32[256]{0:T(256)S(1)}, f32[256,4352]{1,0:T(8,128)S(1)}) fusion(pred[256,4352]{1,0:T(32,128)(4,1)} %get-tuple-element.180, bf16[4352,576]{1,0:T(8,128)(2,1)} %get-tuple-element.179, bf16[256,64]{1,0:T(8,128)(2,1)S(1)} %slice.54, bf16[256,512]{1,0:T(8,128)(2,1)S(1)} %convolution_convert_fusion.3), kind=kOutput, calls=%fused_computation.63.clone.1 | convolution fusion | flops 1287388928 | bytes 10880000 | tf_op jit(solution)/shard_map/while/body/eval_jaxpr/dot_general | solution.py:49
  194.3 2.1 copy-done.2
  197.2 5.1 %fusion.43 = bf16[1,256,128]{2,1,0:T(8,128)(2,1)S(1)} fusion(bf16[4352,512]{1,0:T(8,128)(2,1)} %get-tuple-element.181, f32[256,4352]{1,0:T(8,128)} %copy-done.2, f32[256]{0:T(256)S(1)} %fusion.42, f32[256]{0:T(256)S(1)} %get-tuple-element.156, bf16[8,512,128]{2,1,0:T(8,128)(2,1)} %get-tuple-element.182, s32[]{:T(128)} %get-tuple-element.166), kind=kOutput, calls=%fused_computation.12.clone.1 | convolution fusion | flops 1177911296 | bytes 9112064 | tf_op jit(solution)/shard_map/while/body/eval_jaxpr/dot_general | solution.py:62
  202.5 11.0 %convolution_convert_fusion.1 = bf16[256,7168]{1,0:T(8,128)(2,1)} fusion(bf16[256,1024]{0,1:T(8,128)(2,1)S(1)} %bitcast.69, bf16[1024,7168]{1,0:T(8,128)(2,1)} %param.19), kind=kOutput, calls=%fused_computation.26 | convolution fusion | flops 3759931392 | bytes 18874368 | tf_op jit(solution)/shard_map/dot_general | solution.py:102
  213.5 5.9 %copy.35 = bf16[256,7168]{0,1:T(8,128)(2,1)} copy(bf16[256,7168]{1,0:T(8,128)(2,1)} %convolution_convert_fusion.1) | data formatting | bytes 7340032
  219.4 37.2 %reduce-scatter.4.cloned.1.call-done = bf16[896,256]{1,0:T(8,128)(2,1)} async-done(((bf16[7168,256]{1,0:T(8,128)(2,1)}), bf16[896,256]{1,0:T(8,128)(2,1)}) %reduce-scatter.4.cloned.1.call-update) | async-done | bytes 458768
  (115 shorter events, 36.4 us)
Async XLA Ops:
  6.5 2.4 copy-start
  6.5 33.9 %copy-start.5 = (bf16[256,576]{0,1:T(8,128)(2,1)S(1)}, bf16[256,576]{0,1:T(8,128)(2,1)}, u32[]{:S(2)}) copy-start(bf16[256,576]{0,1:T(8,128)(2,1)} %param.12) | copy-start | bytes 884740
  6.5 34.1 %copy-start.6 = (s32[1,2,32]{2,1,0:T(2,128)S(1)}, s32[1,2,32]{2,1,0:T(2,128)}, u32[]{:S(2)}) copy-start(s32[1,2,32]{2,1,0:T(2,128)} %param.16) | copy-start | bytes 772
  10.7 32.8 %copy-start.3 = (bf16[256,1536]{1,0:T(8,128)(2,1)S(1)}, bf16[256,1536]{1,0:T(8,128)(2,1)}, u32[]{:S(2)}) copy-start(bf16[256,1536]{1,0:T(8,128)(2,1)} %param.11) | copy-start | bytes 2359300
  10.7 33.1 %copy-start.7 = (s32[1,32]{1,0:T(1,128)S(1)}, s32[1,32]{1,0:T(1,128)}, u32[]{:S(2)}) copy-start(s32[1,32]{1,0:T(1,128)} %param.15) | copy-start | bytes 388
  10.7 28.1 %all-to-all-start = ((bf16[16,4,16,576]{3,2,1,0:T(8,128)(2,1)}), bf16[16,4,16,576]{3,2,1,0:T(8,128)(2,1)S(1)}, u32[]{:S(2)}, u32[]{:S(2)}) async-start(bf16[16,4,16,576]{3,2,1,0:T(8,128)(2,1)} %bitcast.7), calls=%async_computation | async-start | bytes 2621440 | tf_op jit(solution)/shard_map/all_to_all | solution.py:87
  18.0 58.0 %all-gather.3.cloned.1.call-start = ((), (), s32[]{:S(2)}) async-start(), calls=%async_computation.2 | async-start | bytes 5898240 | tf_op jit(solution)/shard_map/all_gather | solution.py:89
  40.4 216.3 %reduce-scatter.4.cloned.1.call-start = ((), (), s32[]{:S(2)}) async-start(), calls=%async_computation.3 | async-start | bytes 4128768
  85.0 2.5 copy-start.4
  93.7 2.1 copy-start.2
  108.1 2.1 copy-start.2
  122.5 2.1 copy-start.2
  136.8 2.1 copy-start.2
  151.2 2.1 copy-start.2
  165.6 2.1 copy-start.2
  180.0 2.1 copy-start.2
  194.3 2.1 copy-start.2
  202.5 56.1 %copy-start.1 = (bf16[32,16,576]{2,1,0:T(8,128)(2,1)S(1)}, bf16[32,16,576]{2,1,0:T(8,128)(2,1)}, u32[]{:S(2)}) copy-start(bf16[32,16,576]{2,1,0:T(8,128)(2,1)} %param.13) | copy-start | bytes 1769476
Sparse Core Ops, SparseCore 0:
  40.5 35.5 all-gather.2
  219.6 37.0 reduce-scatter.3
